TPU v7x, 128 devices: a whole 4x4x4 slice. The times are simulated.
128 devices in a mesh: rows: 16 (over z, x), cols: 8 (over y, core).
Axes of the slice: x: 4, y: 4, z: 4, core: 2. Of those that a mesh axis runs over, the one named last changes fastest.
Arguments:
- densities: bfloat16 [6, 8192, 128, 128], P(None, ('rows', 'cols')), may hold values from -6 to 6
- residuals: bfloat16 [6, 8192, 128, 128], P(None, ('rows', 'cols')), may hold values from -32 to 32
- block_pairs: int32 [2, 8192], P(None, ('rows', 'cols')), may hold values from 0 to 1562
- new_owner: int32 [8192], P(('rows', 'cols')), may hold values from -1 to 15, as said below
Outputs:
- owned_blocks: bfloat16 [4096, 128, 128], P(('rows', 'cols'))
- coefficients: float32 [6], replicated
Inputs may be any that keep to these rules, and one draw needn't show every extreme that they name: A live block stays at its index of cols and moves to index new_owner of rows. For each index of cols, every index of rows becomes the owner of exactly 32 blocks, and at most 4 of them come from one device.
All inputs are finite; a program needn't handle non-finite values.
Results may differ from a plain program's by a relative error of at most 0.0019.
Values may be sent and summed in bfloat16 or wider, within the bound.
A program may use at most 128 MiB of HBM per device.

v0:
```python
import math
import jax
import jax.numpy as jnp
from jax import lax
from jax.sharding import Mesh
from jax.sharding import PartitionSpec as P

OWNED = 32
ROWS = ("rows_0", "rows_1")
ROWS_COLS = ("rows_0", "rows_1", "cols_0", "cols_1")
mix_weight = 0.3


def over_axes(shard, axes):
    for axis in axes:
        shard = lax.psum(shard, axis)
    return shard


def sent_together(arrays, axis, split_dim, concat_dim, along):
    widths = [math.prod(a.shape[along:]) for a in arrays]
    both = jnp.concatenate(
        [a.reshape(*a.shape[:along], w) for a, w in zip(arrays, widths)], axis=along
    )
    whole = lax.all_to_all(both, axis, split_axis=split_dim, concat_axis=concat_dim, tiled=True)
    pieces = jnp.split(whole, [sum(widths[:k]) for k in range(1, len(widths))], axis=along)
    return tuple(
        (b.reshape(*whole.shape[:along], *a.shape[along:]) for a, b in zip(arrays, pieces))
    )


def small_solve(system, vector):
    order_n = system.shape[0]
    positions = jnp.arange(order_n, dtype=jnp.int32)
    for step_index in range(order_n):
        column = system[:, step_index] / system[step_index, step_index]
        column = jnp.where(positions > step_index, column, 0.0)
        system = system - column[:, None] * system[step_index][None, :]
        vector = vector - column * vector[step_index]
    solution = jnp.zeros((order_n,), jnp.float32)
    for step_index in reversed(range(order_n)):
        inner = jnp.sum(jnp.where(positions > step_index, system[step_index] * solution, 0.0))
        solution = solution.at[step_index].set(
            (vector[step_index] - inner) / system[step_index, step_index]
        )
    return solution


def slot_correlation(residual_set, weights):
    flattened = residual_set.reshape(residual_set.shape[0], residual_set.shape[1], -1)
    per_slot = jnp.einsum("isn,ksn->sik", flattened, flattened, preferred_element_type=jnp.float32)
    return jnp.einsum("s,sik->ik", weights, per_slot)


def blend_history(density_set, residual_set, coefficients):
    running = jnp.zeros(density_set.shape[1:], jnp.float32)
    for hist_index in range(density_set.shape[0]):
        running = running + coefficients[hist_index] * (
            density_set[hist_index].astype(jnp.float32)
            + mix_weight * residual_set[hist_index].astype(jnp.float32)
        )
    return running.astype(jnp.bfloat16)


def compact_order(arrived_weights):
    usable = arrived_weights > 0.0
    position = jnp.cumsum(usable.astype(jnp.int32)) - 1
    spots = jnp.where(usable, position, OWNED)
    count_in = arrived_weights.shape[0]
    return (
        jnp.zeros((OWNED,), jnp.int32)
        .at[spots]
        .set(jnp.arange(count_in, dtype=jnp.int32), mode="drop")
    )


def on_device(densities, residuals, block_pairs, new_owner):
    rows_count = lax.axis_size(ROWS)
    held_slots = new_owner.shape[0]
    pair_cap = 2 * OWNED // rows_count
    sent_count = rows_count * pair_cap
    alive_slot = new_owner >= 0
    weights = jnp.where(
        alive_slot, jnp.where(block_pairs[0] == block_pairs[1], 1.0, 2.0), 0.0
    ).astype(jnp.float32)
    owner_rows = jnp.where(alive_slot, new_owner, rows_count)
    onehot = (owner_rows[:, None] == jnp.arange(rows_count, dtype=jnp.int32)[None, :]).astype(
        jnp.int32
    )
    ranking = jnp.sum(jnp.cumsum(onehot, axis=0) * onehot, axis=1) - 1
    placing = jnp.where(alive_slot, owner_rows * pair_cap + ranking, sent_count)
    slot_table = (
        jnp.full((sent_count,), held_slots, jnp.int32)
        .at[placing]
        .set(jnp.arange(held_slots, dtype=jnp.int32), mode="drop")
    )
    chosen = jnp.minimum(slot_table, held_slots - 1)
    sent_weights = jnp.where(slot_table < held_slots, weights[chosen], 0.0).astype(jnp.bfloat16)
    partial_correlation = slot_correlation(residuals, weights)
    correlation = over_axes(partial_correlation, ROWS_COLS)
    solved = small_solve(correlation, jnp.ones((correlation.shape[0],), jnp.float32))
    coefficients = solved / jnp.sum(solved)
    mixed_blocks = blend_history(densities, residuals, coefficients)
    arrived = sent_together((jnp.take(mixed_blocks, chosen, axis=0), sent_weights), ROWS, 0, 0, 1)
    ordering = compact_order(arrived[1].astype(jnp.float32))
    owned_blocks = jnp.take(arrived[0], ordering, axis=0)
    return (owned_blocks, coefficients)


def solution(mesh):
    finer = Mesh(mesh.devices.reshape(4, 4, 4, 2), ("rows_0", "rows_1", "cols_0", "cols_1"))
    placed = (
        P(None, ROWS_COLS, None, None),
        P(None, ROWS_COLS, None, None),
        P(None, ROWS_COLS),
        P(ROWS_COLS),
    )
    return jax.shard_map(
        on_device,
        mesh=finer,
        in_specs=placed,
        out_specs=(P(ROWS_COLS, None, None), P()),
        check_vma=False,
    )
```

profile of v0, /device:TPU:0, one launch (start us, length us, event | category | flops | bytes accessed | tf_op | source)
XLA Modules:
  0.0 182.0 jit_solution(14039004211042699980)
XLA Ops:
  0.6 19.3 %reshape.282 = bf16[6,64,16384]{2,1,0:T(8,128)(2,1)} reshape(bf16[6,64,128,128]{3,2,1,0:T(8,128)(2,1)} %param.17) | data formatting | bytes 25165824 | tf_op jit(solution)/shard_map/reshape | solution.py:50
  20.0 25.8 %fusion = bf16[64,6,6]{2,1,0:T(8,128)(2,1)S(1)} fusion(bf16[6,64,16384]{2,1,0:T(8,128)(2,1)} %reshape.282), kind=kOutput, calls=%fused_computation.5 | convolution fusion | flops 75497472 | bytes 12587520 | tf_op jit(solution)/shard_map/isn,ksn->sik/dot_general | solution.py:51
  45.9 11.9 %psum.28 = f32[6,6]{1,0:T(8,128)S(1)} all-reduce(f32[6,6]{1,0:T(8,128)S(1)} %bitcast.87), channel_id=1, replica_groups=mesh['rows_0'=4,'rows_1'=4,'cols_0'=4,'cols_1'=2] {'rows_0'}, use_global_device_ids=true, to_apply=%region_3.4 | all-reduce | flops 36 | bytes 288 | tf_op jit(solution)/shard_map/psum | solution.py:16
  57.8 10.5 %psum.29 = f32[6,6]{1,0:T(8,128)S(1)} all-reduce(f32[6,6]{1,0:T(8,128)S(1)} %psum.28), channel_id=1, replica_groups=mesh['rows_0'=4,'rows_1'=4,'cols_0'=4,'cols_1'=2] {'rows_1'}, use_global_device_ids=true, to_apply=%region_4.5 | all-reduce | flops 36 | bytes 288 | tf_op jit(solution)/shard_map/psum | solution.py:16
  68.3 10.7 %psum.30 = f32[6,6]{1,0:T(8,128)S(1)} all-reduce(f32[6,6]{1,0:T(8,128)S(1)} %psum.29), channel_id=1, replica_groups=mesh['rows_0'=4,'rows_1'=4,'cols_0'=4,'cols_1'=2] {'cols_0'}, use_global_device_ids=true, to_apply=%region_5.6 | all-reduce | flops 36 | bytes 288 | tf_op jit(solution)/shard_map/psum | solution.py:16
  79.0 2.5 %psum.31 = f32[6,6]{1,0:T(8,128)S(1)} all-reduce(f32[6,6]{1,0:T(8,128)S(1)} %psum.30), channel_id=1, replica_groups=mesh['rows_0'=4,'rows_1'=4,'cols_0'=4,'cols_1'=2] {'cols_1'}, use_global_device_ids=true, to_apply=%region_6.7 | all-reduce | flops 36 | bytes 288 | tf_op jit(solution)/shard_map/psum | solution.py:16
  82.0 0.8 fusion.7
  82.8 0.6 slice.248
  83.4 0.8 select_reduce_fusion.5
  84.4 0.6 slice.252
  84.9 0.8 select_reduce_fusion.4
  85.8 0.6 slice.256
  86.4 0.8 select_reduce_fusion.3
  87.3 0.6 slice.260
  87.9 0.8 select_reduce_fusion.2
  88.8 0.6 slice.264
  89.4 0.8 select_reduce_fusion.1
  90.3 0.7 fusion.38
  91.0 0.7 fusion.30
  91.7 0.6 slice.249
  92.3 0.6 fusion.17
  93.5 0.6 fusion.20
  94.7 0.6 fusion.23
  96.0 0.6 fusion.26
  97.2 0.6 fusion.29
  97.9 0.7 fusion.40
  100.6 0.8 fusion.27
  103.3 0.6 fusion.24
  105.8 0.7 fusion.21
  108.4 0.6 fusion.18
  111.0 0.6 fusion.15
  113.6 0.6 reduce_sum.79
  114.2 0.6 broadcast_divide_fusion
  114.9 0.7 fusion.39
  115.9 1.0 scatter_custom_fusion
  116.9 0.8 gather_fusion.1
  117.7 15.0 %fusion.2 = bf16[64,128,128]{2,1,0:T(8,128)(2,1)S(1)} fusion(bf16[6,64,128,128]{3,2,1,0:T(8,128)(2,1)} %param.17, bf16[6,64,128,128]{3,2,1,0:T(8,128)(2,1)} %param.16, f32[]{:T(128)} %bitcast.49, f32[]{:T(128)} %bitcast.48, f32[]{:T(128)} %bitcast.47, f32[]{:T(128)} %bitcast.46, f32[]{:T(128)} %bitcast.45, f32[]{:T(128)} %bitcast.44), kind=kLoop, calls=%fused_computation.11 | loop fusion | flops 37748736 | bytes 27263000 | tf_op jit(solution)/shard_map/convert_element_type | solution.py:62
  132.7 2.2 %gather_fusion = bf16[64,128,128]{2,1,0:T(8,128)(2,1)} fusion(bf16[64,128,128]{2,1,0:T(8,128)(2,1)S(1)} %fusion.2, s32[1024]{0:T(1024)S(1)} %pad_clamp_fusion.1), kind=kCustom, calls=%fused_computation | custom fusion | bytes 4194560 | tf_op jit(solution)/shard_map/jit(_take)/gather | solution.py:104
  134.9 2.6 %gather.14 = bf16[16,4,16384]{2,1,0:T(4,128)(2,1)S(1)} reshape(bf16[64,128,128]{2,1,0:T(8,128)(2,1)} %gather_fusion) | data formatting | bytes 4194304 | tf_op jit(solution)/shard_map/jit(_take)/gather | solution.py:104
  137.8 1.0 broadcast_select_fusion
  138.8 1.0 pad_maximum_fusion
  139.7 32.8 %all_to_all.9 = bf16[16,4,16385]{2,1,0:T(4,128)(2,1)} all-to-all(bf16[16,4,16385]{2,1,0:T(4,128)(2,1)S(1)} %pad_maximum_fusion), channel_id=1, replica_groups=mesh['rows_0'=4,'rows_1'=4,'cols_0'=4,'cols_1'=2] {'rows_0','rows_1'}, dimensions={0} | all-to-all | bytes 4194560 | tf_op jit(solution)/shard_map/all_to_all | solution.py:25
  172.5 2.8 %all_to_all.7 = bf16[64,16385]{1,0:T(8,128)(2,1)S(1)} reshape(bf16[16,4,16385]{2,1,0:T(4,128)(2,1)} %all_to_all.9) | data formatting | bytes 4194560 | tf_op jit(solution)/shard_map/all_to_all | solution.py:25
  175.4 1.5 slice_bitcast_fusion
  177.1 0.8 scatter_custom_fusion.1
  177.9 2.2 %copy.11 = bf16[8,8,128,128]{3,2,1,0:T(8,128)(2,1)S(1)} copy(bf16[8,8,128,128]{3,1,2,0:T(8,128)(2,1)} %slice_bitcast_fusion) | data formatting | bytes 4194304
  180.1 0.8 gather_fusion.2
  180.8 1.1 broadcast_select_fusion.1
  (51 shorter events, 4.5 us)
Async XLA Ops:
  20.0 25.8 %copy-start.1 = (s32[2,64]{1,0:T(2,128)S(1)}, s32[2,64]{1,0:T(2,128)}, u32[]{:S(2)}) copy-start(s32[2,64]{1,0:T(2,128)} %param.18) | copy-start | bytes 1540
  20.0 25.8 %copy-start.2 = (s32[64]{0:T(128)S(1)}, s32[64]{0:T(128)}, u32[]{:S(2)}) copy-start(s32[64]{0:T(128)} %param.19) | copy-start | bytes 772
  114.9 17.8 %copy-start = (f32[6]{0:T(128)}, f32[6]{0:T(128)S(1)}, u32[]{:S(2)}) copy-start(f32[6]{0:T(128)S(1)} %broadcast_divide_fusion) | copy-start | bytes 76
where the time goes:
time: 183 us; the launch traced here: 182 us
  blocking collectives  68.4 us (37%)
  local copies, waits for them, and re-layouts  42.7 us (23%)
  other arithmetic  32.5 us (18%)
  matrix products  25.9 us (14%)
  between operations  12.5 us (7%)
    psum x4, blocking collectives, over_axes(): shard = lax.psum(shard, axis)  35.5 us
    all_to_all x1, blocking collectives, sent_together(): lax.all_to_all(both, axis, split_axis=split_dim, concat_axis=concat_dim,...  32.8 us
    dot_general x1, matrix products, slot_correlation(): jnp.einsum('isn,ksn->sik', flattened, flattened, preferred_element_type=j...  25.8 us
    reshape x1, local copies, waits for them, and re-layouts, slot_correlation(): residual_set.reshape(residual_set.shape[0], residual_set.shape[1], -1)  19.3 us
    convert_element_type x1, other arithmetic, blend_history(): return running.astype(jnp.bfloat16)  15 us
    gather x2, local copies, waits for them, and re-layouts, on_device(): jnp.take(mixed_blocks, chosen, axis=0)  4.79 us
    select_n x5, other arithmetic, small_solve(): column = jnp.where(positions > step_index, column, 0.0)  4.13 us
    reduce_sum x6, other arithmetic, small_solve(): jnp.sum(jnp.where(positions > step_index, system[step_index] * solution,...  3.92 us

commit v1 on v0

--- a/solution.py
+++ b/solution.py
@@ -13,7 +13,7 @@
 
 def over_axes(shard, axes):
     for axis in axes:
-        shard = lax.psum(shard, axis)
+        shard = jnp.sum(lax.all_gather(shard, axis_name=axis), axis=0)
     return shard
 
 

time: 183 us -> 190 us (1.038)
  blocking collectives: 68.4 us -> 75.1 us
    all_gather x0 -> x4, blocking collectives: none -> 40 us  [over_axes(): shard = jnp.sum(lax.all_gather(shard, axis_name=axis), axis=0)]
    psum x4 -> x0, blocking collectives: 35.5 us -> none  [over_axes(): shard = lax.psum(shard, axis)]
    all_to_all x1, blocking collectives: 32.8 us -> 35 us  [sent_together(): lax.all_to_all(both, axis, split_axis=split_dim, concat_axis=concat_dim,...]
where the time goes in v1:
time: 190 us; the launch traced here: 189 us
  blocking collectives  75.1 us (40%)
  local copies, waits for them, and re-layouts  42.7 us (22%)
  other arithmetic  32.5 us (17%)
  matrix products  25.9 us (14%)
  between operations  12.5 us (7%)
    all_gather x4, blocking collectives, over_axes(): shard = jnp.sum(lax.all_gather(shard, axis_name=axis), axis=0)  40 us
    all_to_all x1, blocking collectives, sent_together(): lax.all_to_all(both, axis, split_axis=split_dim, concat_axis=concat_dim,...  35 us
    dot_general x1, matrix products, slot_correlation(): jnp.einsum('isn,ksn->sik', flattened, flattened, preferred_element_type=j...  25.8 us
    reshape x1, local copies, waits for them, and re-layouts, slot_correlation(): residual_set.reshape(residual_set.shape[0], residual_set.shape[1], -1)  19.3 us
    convert_element_type x1, other arithmetic, blend_history(): return running.astype(jnp.bfloat16)  15 us
    gather x2, local copies, waits for them, and re-layouts, on_device(): jnp.take(mixed_blocks, chosen, axis=0)  4.79 us
    select_n x5, other arithmetic, small_solve(): column = jnp.where(positions > step_index, column, 0.0)  4.13 us
    reduce_sum x6, other arithmetic, small_solve(): jnp.sum(jnp.where(positions > step_index, system[step_index] * solution,...  3.92 us

profile of v1, /device:TPU:0, one launch (start us, length us, event | category | flops | bytes accessed | tf_op | source)
XLA Modules:
  0.0 188.7 jit_solution(14205851705961004455)
XLA Ops:
  0.6 19.3 %reshape.282 = bf16[6,64,16384]{2,1,0:T(8,128)(2,1)} reshape(bf16[6,64,128,128]{3,2,1,0:T(8,128)(2,1)} %param.17) | data formatting | bytes 25165824 | tf_op jit(solution)/shard_map/reshape | solution.py:50
  20.0 25.8 %fusion = bf16[64,6,6]{2,1,0:T(8,128)(2,1)S(1)} fusion(bf16[6,64,16384]{2,1,0:T(8,128)(2,1)} %reshape.282), kind=kOutput, calls=%fused_computation.5 | convolution fusion | flops 75497472 | bytes 12587520 | tf_op jit(solution)/shard_map/isn,ksn->sik/dot_general | solution.py:51
  45.9 13.3 %all-gather.4 = f32[4,6,6]{2,1,0:T(8,128)S(1)} all-gather(f32[1,6,6]{2,1,0:T(8,128)S(1)} %copy.12), channel_id=2, replica_groups=mesh['rows_0'=4,'rows_1'=4,'cols_0'=4,'cols_1'=2] {'rows_0'}, dimensions={0}, use_global_device_ids=true | all-gather | bytes 720 | tf_op jit(solution)/shard_map/all_gather | solution.py:16
  59.2 12.4 %all-gather.5 = f32[4,6,6]{2,1,0:T(8,128)S(1)} all-gather(f32[1,6,6]{2,1,0:T(8,128)S(1)} %bitcast.88), channel_id=3, replica_groups=mesh['rows_0'=4,'rows_1'=4,'cols_0'=4,'cols_1'=2] {'rows_1'}, dimensions={0}, use_global_device_ids=true | all-gather | bytes 720 | tf_op jit(solution)/shard_map/all_gather | solution.py:16
  71.6 12.5 %all-gather.6 = f32[4,6,6]{2,1,0:T(8,128)S(1)} all-gather(f32[1,6,6]{2,1,0:T(8,128)S(1)} %bitcast.89), channel_id=4, replica_groups=mesh['rows_0'=4,'rows_1'=4,'cols_0'=4,'cols_1'=2] {'cols_0'}, dimensions={0}, use_global_device_ids=true | all-gather | bytes 720 | tf_op jit(solution)/shard_map/all_gather | solution.py:16
  84.2 1.8 all-gather.7
  86.5 0.8 fusion.7
  87.4 0.6 slice.248
  88.0 0.8 select_reduce_fusion.5
  88.9 0.6 slice.252
  89.5 0.8 select_reduce_fusion.4
  90.4 0.6 slice.256
  91.0 0.8 select_reduce_fusion.3
  91.9 0.6 slice.260
  92.5 0.8 select_reduce_fusion.2
  93.4 0.6 slice.264
  94.0 0.8 select_reduce_fusion.1
  94.9 0.7 fusion.38
  95.6 0.7 fusion.30
  96.2 0.6 slice.249
  96.8 0.6 fusion.17
  98.0 0.6 fusion.20
  99.3 0.6 fusion.23
  100.5 0.6 fusion.26
  101.8 0.6 fusion.29
  102.4 0.7 fusion.40
  105.1 0.8 fusion.27
  107.9 0.6 fusion.24
  110.4 0.7 fusion.21
  113.0 0.6 fusion.18
  115.5 0.6 fusion.15
  118.1 0.6 reduce_sum.119
  118.7 0.6 broadcast_divide_fusion
  119.4 0.7 fusion.39
  120.5 1.0 scatter_custom_fusion
  121.4 0.8 gather_fusion.1
  122.2 15.0 %fusion.2 = bf16[64,128,128]{2,1,0:T(8,128)(2,1)S(1)} fusion(bf16[6,64,128,128]{3,2,1,0:T(8,128)(2,1)} %param.17, bf16[6,64,128,128]{3,2,1,0:T(8,128)(2,1)} %param.16, f32[]{:T(128)} %bitcast.52, f32[]{:T(128)} %bitcast.51, f32[]{:T(128)} %bitcast.50, f32[]{:T(128)} %bitcast.49, f32[]{:T(128)} %bitcast.48, f32[]{:T(128)} %bitcast.47), kind=kLoop, calls=%fused_computation.11 | loop fusion | flops 37748736 | bytes 27263000 | tf_op jit(solution)/shard_map/convert_element_type | solution.py:62
  137.2 2.2 %gather_fusion = bf16[64,128,128]{2,1,0:T(8,128)(2,1)} fusion(bf16[64,128,128]{2,1,0:T(8,128)(2,1)S(1)} %fusion.2, s32[1024]{0:T(1024)S(1)} %pad_clamp_fusion.1), kind=kCustom, calls=%fused_computation | custom fusion | bytes 4194560 | tf_op jit(solution)/shard_map/jit(_take)/gather | solution.py:104
  139.4 2.6 %gather.14 = bf16[16,4,16384]{2,1,0:T(4,128)(2,1)S(1)} reshape(bf16[64,128,128]{2,1,0:T(8,128)(2,1)} %gather_fusion) | data formatting | bytes 4194304 | tf_op jit(solution)/shard_map/jit(_take)/gather | solution.py:104
  142.3 1.0 broadcast_select_fusion
  143.3 1.0 pad_maximum_fusion
  144.3 35.0 %all_to_all.9 = bf16[16,4,16385]{2,1,0:T(4,128)(2,1)} all-to-all(bf16[16,4,16385]{2,1,0:T(4,128)(2,1)S(1)} %pad_maximum_fusion), channel_id=1, replica_groups=mesh['rows_0'=4,'rows_1'=4,'cols_0'=4,'cols_1'=2] {'rows_0','rows_1'}, dimensions={0} | all-to-all | bytes 4194560 | tf_op jit(solution)/shard_map/all_to_all | solution.py:25
  179.3 2.8 %all_to_all.7 = bf16[64,16385]{1,0:T(8,128)(2,1)S(1)} reshape(bf16[16,4,16385]{2,1,0:T(4,128)(2,1)} %all_to_all.9) | data formatting | bytes 4194560 | tf_op jit(solution)/shard_map/all_to_all | solution.py:25
  182.1 1.5 slice_bitcast_fusion
  183.9 0.8 scatter_custom_fusion.1
  184.7 2.2 %copy.13 = bf16[8,8,128,128]{3,2,1,0:T(8,128)(2,1)S(1)} copy(bf16[8,8,128,128]{3,1,2,0:T(8,128)(2,1)} %slice_bitcast_fusion) | data formatting | bytes 4194304
  186.9 0.8 gather_fusion.2
  187.6 1.1 broadcast_select_fusion.1
  (55 shorter events, 4.5 us)
Async XLA Ops:
  20.0 25.8 %copy-start.1 = (s32[2,64]{1,0:T(2,128)S(1)}, s32[2,64]{1,0:T(2,128)}, u32[]{:S(2)}) copy-start(s32[2,64]{1,0:T(2,128)} %param.18) | copy-start | bytes 1540
  20.0 25.8 %copy-start.2 = (s32[64]{0:T(128)S(1)}, s32[64]{0:T(128)}, u32[]{:S(2)}) copy-start(s32[64]{0:T(128)} %param.19) | copy-start | bytes 772
  119.4 17.8 %copy-start = (f32[6]{0:T(128)}, f32[6]{0:T(128)S(1)}, u32[]{:S(2)}) copy-start(f32[6]{0:T(128)S(1)} %broadcast_divide_fusion) | copy-start | bytes 76
